TPU v7x, 32 devices: a whole 2x2x4 slice. The times are simulated.
32 devices in a mesh: dp: 8 (over z, x), expert: 4 (over y, core).
Axes of the slice: x: 2, y: 2, z: 4, core: 2. Of those that a mesh axis runs over, the one named last changes fastest.
Arguments:
- local_grads: bfloat16 [8, 4, 4, 524288], P('dp', 'expert')
- master_weights: float32 [4, 4, 524288], P('expert', None, 'dp'), may hold values from -6 to 6
- first_moment: float32 [4, 4, 524288], P('expert', None, 'dp')
- second_moment: float32 [4, 4, 524288], P('expert', None, 'dp')
Outputs:
- new_params: bfloat16 [4, 4, 524288], P('expert')
- new_master: float32 [4, 4, 524288], P('expert', None, 'dp')
- new_first: float32 [4, 4, 524288], P('expert', None, 'dp')
- new_second: float32 [4, 4, 524288], P('expert', None, 'dp')
All inputs are finite; a program needn't handle non-finite values.
Results may differ from a plain program's by a relative error of at most 0.0013.
Values may be sent and summed in bfloat16 or wider, within the bound.
A program may use at most 128 MiB of HBM per device.

v0:
```python
import jax
import jax.numpy as jnp
from jax import lax
from jax.sharding import PartitionSpec as P

beta_first = 0.9
beta_second = 0.95
correct_first = 1.0 - 0.9**10
correct_second = 1.0 - 0.95**10
learn_rate = 0.05
decay_rate = 0.1
clip_limit = 1.0
tiny_eps = 1e-08
norm_eps = 1e-06


def adam_update(gradient, master, first, second, clip_factor):
    scaled = clip_factor * gradient
    new_first = beta_first * first + (1.0 - beta_first) * scaled
    new_second = beta_second * second + (1.0 - beta_second) * scaled * scaled
    direction = new_first / correct_first / (jnp.sqrt(new_second / correct_second) + tiny_eps)
    new_master = master - learn_rate * (decay_rate * master + direction)
    return (new_master, new_first, new_second)


def shards(local_grads, master_weights, first_moment, second_moment):
    replicas = lax.axis_size("dp")
    own_grads = local_grads[0, 0]
    layer_count = own_grads.shape[0]
    share = own_grads.shape[1] // replicas
    pieces_all = own_grads.reshape(layer_count, replicas, share)
    arrived = lax.all_to_all(pieces_all, "dp", split_axis=1, concat_axis=1, tiled=True)
    reduced = jnp.sum(arrived.astype(jnp.float32), axis=1)
    mean_grad = reduced / replicas
    squares = jnp.sum(mean_grad * mean_grad)
    total_squares = lax.psum(squares, ("dp", "expert"))
    grad_norm = jnp.sqrt(total_squares)
    clip_factor = jnp.minimum(1.0, clip_limit / (grad_norm + norm_eps))
    new_master, new_first, new_second = adam_update(
        mean_grad, master_weights[0], first_moment[0], second_moment[0], clip_factor
    )
    rounded = new_master.astype(jnp.bfloat16)
    gathered = lax.all_gather(rounded, "dp", axis=1, tiled=True)
    return (gathered[None], new_master[None], new_first[None], new_second[None])


def solution(mesh):
    placed = (
        P("dp", "expert", None, None),
        P("expert", None, "dp"),
        P("expert", None, "dp"),
        P("expert", None, "dp"),
    )
    return jax.shard_map(
        shards,
        mesh=mesh,
        in_specs=placed,
        out_specs=(
            P("expert", None, None),
            P("expert", None, "dp"),
            P("expert", None, "dp"),
            P("expert", None, "dp"),
        ),
        check_vma=False,
    )
```

profile of v0, /device:TPU:0, one launch (start us, length us, event | category | flops | bytes accessed | tf_op | source)
XLA Modules:
  0.0 239.4 jit_solution(7856903270646459027)
XLA Ops:
  7.2 0.0 all-gather.2.cloned.1.call-start
  7.2 100.5 %all_to_all.5 = bf16[4,8,65536]{2,0,1:T(4,128)(2,1)S(1)} all-to-all(bf16[4,8,65536]{2,0,1:T(4,128)(2,1)} %bitcast.32), channel_id=1, replica_groups=mesh['dp'=8,'expert'=4] {'dp'}, dimensions={1} | all-to-all | bytes 8388608 | tf_op jit(solution)/shard_map/all_to_all | solution.py:32
  107.7 0.0 copy-start
  107.7 0.0 copy-start.1
  107.7 1.9 convert_reduce_fusion
  109.6 1.1 multiply_reduce_fusion
  110.7 38.9 %psum.7 = f32[]{:T(128)} all-reduce(f32[]{:T(128)} %multiply_reduce_fusion), channel_id=1, replica_groups=mesh['dp'=8,'expert'=4] {'dp','expert'}, use_global_device_ids=true, to_apply=%region_2.0 | all-reduce | flops 1 | bytes 8 | tf_op jit(solution)/shard_map/psum | solution.py:36
  150.3 0.0 copy-done
  150.3 0.0 copy-done.1
  150.4 3.7 %fusion.10 = bf16[4,65536]{1,0:T(4,128)(2,1)} fusion(f32[1,4,65536]{2,1,0:T(4,128)S(1)} %copy-done, f32[1,4,65536]{2,1,0:T(4,128)S(1)} %copy-done.1, f32[1,4,65536]{2,1,0:T(4,128)} %param.6, f32[4,65536]{1,0:T(4,128)S(1)} %convert_reduce_fusion, f32[]{:T(128)S(6)} %mul.104), kind=kLoop, calls=%fused_computation.17 | loop fusion | flops 4456448 | bytes 4718596 | tf_op jit(solution)/shard_map/convert_element_type | solution.py:42
  154.1 0.0 all-gather.2.cloned.1.call-update
  154.1 4.5 %multiply_subtract_fusion = (f32[1,4,65536]{2,1,0:T(4,128)}, f32[1,4,65536]{2,1,0:T(4,128)}, f32[1,4,65536]{2,1,0:T(4,128)}) fusion(f32[1,4,65536]{2,1,0:T(4,128)S(1)} %copy-done, f32[4,65536]{1,0:T(4,128)S(1)} %convert_reduce_fusion, f32[]{:T(128)S(6)} %mul.104, f32[1,4,65536]{2,1,0:T(4,128)} %param.6, f32[1,4,65536]{2,1,0:T(4,128)S(1)} %copy-done.1), kind=kLoop, calls=%fused_computation.18 | loop fusion | flops 4194304 | bytes 7340036 | tf_op jit(solution)/shard_map/sub | solution.py:22
  158.6 68.7 %all-gather.2.cloned.1.call-done = bf16[4,524288]{1,0:T(4,128)(2,1)} async-done(((bf16[4,65536]{1,0:T(4,128)(2,1)}), bf16[4,524288]{1,0:T(4,128)(2,1)}) %all-gather.2.cloned.1.call-update) | async-done | bytes 4194320 | tf_op jit(solution)/shard_map/all_gather | solution.py:43
  227.2 5.3 %copy.9 = bf16[1,4,524288]{2,1,0:T(4,128)(2,1)} copy(bf16[1,4,524288]{2,1,0:T(4,128)(2,1)} %bitcast.33) | data formatting | bytes 8388608
Async XLA Ops:
  7.2 220.1 %all-gather.2.cloned.1.call-start = ((), (), s32[]{:S(2)}) async-start(), calls=%async_computation.1 | async-start | bytes 4718592 | tf_op jit(solution)/shard_map/all_gather | solution.py:43
  107.7 42.7 %copy-start = (f32[1,4,65536]{2,1,0:T(4,128)S(1)}, f32[1,4,65536]{2,1,0:T(4,128)}, u32[]{:S(2)}) copy-start(f32[1,4,65536]{2,1,0:T(4,128)} %param.5) | copy-start | bytes 3145732
  107.7 42.7 %copy-start.1 = (f32[1,4,65536]{2,1,0:T(4,128)S(1)}, f32[1,4,65536]{2,1,0:T(4,128)}, u32[]{:S(2)}) copy-start(f32[1,4,65536]{2,1,0:T(4,128)} %param.7) | copy-start | bytes 3145732
Sparse Core Ops, SparseCore 0:
  154.2 72.9 all-gather.1
where the time goes:
time: 240 us; the launch traced here: 239 us
  blocking collectives  139 us (58%)
  waiting for transfers between devices  68.7 us (29%)
  between operations  14.8 us (6%)
  other arithmetic  11.2 us (5%)
  local copies, waits for them, and re-layouts  5.29 us (2%)
    all_to_all x1, blocking collectives, shards(): lax.all_to_all(pieces_all, 'dp', split_axis=1, concat_axis=1, tiled=True)  100 us
    all_gather x1, waiting for transfers between devices, shards(): gathered = lax.all_gather(rounded, 'dp', axis=1, tiled=True)  68.7 us
    psum x1, blocking collectives, shards(): total_squares = lax.psum(squares, ('dp', 'expert'))  38.9 us
    unnamed x5, local copies, waits for them, and re-layouts  5.29 us
  transfers between devices with their start and end apart: 1, of which 1 were waited for; matrix products, arithmetic and copies ran while one was open for 2% of the time, Pallas kernels for 0%

commit v1 on v0

v1 whole, which is shorter than its diff:
```python
import functools

import jax
import jax.numpy as jnp
from jax import lax
from jax.experimental import pallas as pl
from jax.experimental.pallas import tpu as pltpu
from jax.sharding import PartitionSpec as P

beta_first = 0.9
beta_second = 0.95
correct_first = 1.0 - 0.9**10
correct_second = 1.0 - 0.95**10
learn_rate = 0.05
decay_rate = 0.1
clip_limit = 1.0
tiny_eps = 1e-08
norm_eps = 1e-06

MESH = pl.DeviceIdType.MESH
F32 = jnp.float32
CHUNKS = 4
BLOCK = 2048


def adam_update(gradient, master, first, second, clip_factor):
    scaled = clip_factor * gradient
    new_first = beta_first * first + (1.0 - beta_first) * scaled
    new_second = beta_second * second + (1.0 - beta_second) * scaled * scaled
    direction = new_first / correct_first / (jnp.sqrt(new_second / correct_second) + tiny_eps)
    new_master = master - learn_rate * (decay_rate * master + direction)
    return (new_master, new_first, new_second)


def kernel(
    Z, X, E, share,
    grads, master_in, first_in, second_in,
    params_out, master_out, first_out, second_out,
    own, xr, low, high, sbuf, master, first, second, gathered, norms, norms2,
    own_sem, state_sem, out_sem, x_send, x_recv, z_send, low_recv, high_recv,
    n_send, n_recv, m_send, m_recv, g_send, g_recv, p_sem,
):
    n = Z * X
    dp = lax.axis_index("dp")
    ex = lax.axis_index("expert")
    z, x = dp // X, dp % X
    chunk = share // CHUNKS

    def at_dp(zz, xx):
        return (zz * X + xx, ex)

    def lanes(base, size):
        return pl.ds(pl.multiple_of(base, 128), size)

    barrier = pltpu.get_barrier_semaphore()
    for k in range(1, n):
        pl.semaphore_signal(barrier, inc=1, device_id=((dp + k) % n, ex), device_id_type=MESH)
    for k in range(1, E):
        pl.semaphore_signal(barrier, inc=1, device_id=(dp, (ex + k) % E), device_id_type=MESH)
    pl.semaphore_wait(barrier, n - 1 + E - 1)

    def own_copy(zz):
        return pltpu.make_async_copy(
            grads.at[:, lanes((zz * X + x) * share, share)], own.at[zz], own_sem.at[zz]
        )

    def x_copy(zz, k, c):
        to = (x + k) % X
        return pltpu.make_async_remote_copy(
            src_ref=grads.at[:, lanes((zz * X + to) * share + c * chunk, chunk)],
            dst_ref=xr.at[zz, k - 1, :, lanes(c * chunk, chunk)],
            send_sem=x_send.at[zz, k - 1, c],
            recv_sem=x_recv.at[zz, k - 1, c],
            device_id=at_dp(z, to),
            device_id_type=MESH,
        )

    def for_dest(k, act):
        @pl.when(z + k < Z)
        def _():
            act(z + k)

        if k:
            @pl.when(z - k >= 0)
            def _():
                act(z - k)

    def start_first(zz):
        own_copy(zz).start()

        def body(c, carry):
            for k in range(1, X):
                x_copy(zz, k, c).start()
            return carry

        lax.fori_loop(0, CHUNKS, body, 0)

    for k in range(Z - 1, -1, -1):
        for_dest(k, start_first)
    states = [
        pltpu.make_async_copy(a, b, state_sem.at[i])
        for i, (a, b) in enumerate(((master_in, master), (first_in, first), (second_in, second)))
    ]
    for s in states:
        s.start()

    def z_copy(zz, c, up):
        where = lanes(c * chunk, chunk)
        return pltpu.make_async_remote_copy(
            src_ref=sbuf.at[zz, :, where],
            dst_ref=(low if up else high).at[zz, :, where],
            send_sem=z_send.at[zz, c],
            recv_sem=(low_recv if up else high_recv).at[zz, c],
            device_id=at_dp(z + 1 if up else z - 1, x),
            device_id_type=MESH,
        )

    def sum_block(zz, where, extras):
        total = own[zz, :, where].astype(F32)
        for k in range(1, X):
            total = total + xr[zz, k - 1, :, where].astype(F32)
        for r in extras:
            total = total + r[zz, :, where]
        return total

    def add_chunk(zz, c, extras):
        def body(b, carry):
            where = lanes(c * chunk + b * BLOCK, BLOCK)
            sbuf[zz, :, where] = sum_block(zz, where, extras)
            return carry

        lax.fori_loop(0, chunk // BLOCK, body, 0)

    def hop(zz, c, up):
        for k in range(1, X):
            x_copy(zz, k, c).wait_recv()
        edge = z == (0 if up else Z - 1)

        @pl.when(edge)
        def _():
            add_chunk(zz, c, ())

        @pl.when(jnp.logical_not(edge))
        def _():
            z_copy(zz, c, up).wait_recv()
            add_chunk(zz, c, (low if up else high,))

        z_copy(zz, c, up).start()

    for k in range(Z - 1, 0, -1):
        for_dest(k, lambda zz: own_copy(zz).wait())

        def body(c, carry, k=k):
            @pl.when(z + k < Z)
            def _():
                hop(z + k, c, True)

            @pl.when(z - k >= 0)
            def _():
                hop(z - k, c, False)

            return carry

        lax.fori_loop(0, CHUNKS, body, 0)

    own_copy(z).wait()
    norms2[0] = jnp.zeros((8, 128), F32)

    def finish_chunk(c, extras):
        def body(b, carry):
            where = lanes(c * chunk + b * BLOCK, BLOCK)
            mean = sum_block(z, where, extras) / n
            sbuf[z, :, where] = mean
            return carry + mean * mean

        squares = lax.fori_loop(0, chunk // BLOCK, body, jnp.zeros((own.shape[1], BLOCK), F32))
        norms2[0] = norms2[0] + jnp.full((8, 128), jnp.sum(squares), F32)

    def finish(c, carry):
        for k in range(1, X):
            x_copy(z, k, c).wait_recv()

        @pl.when(z > 0)
        def _():
            z_copy(z, c, True).wait_recv()

        @pl.when(z < Z - 1)
        def _():
            z_copy(z, c, False).wait_recv()

        @pl.when(z == 0)
        def _():
            finish_chunk(c, (high,))

        @pl.when(z == Z - 1)
        def _():
            finish_chunk(c, (low,))

        @pl.when(jnp.logical_and(z > 0, z < Z - 1))
        def _():
            finish_chunk(c, (low, high))

        return carry

    lax.fori_loop(0, CHUNKS, finish, 0)

    norms[0] = norms2[0]

    def n_copy(k):
        return pltpu.make_async_remote_copy(
            src_ref=norms.at[0], dst_ref=norms.at[k],
            send_sem=n_send.at[k], recv_sem=n_recv.at[k],
            device_id=((dp + k) % n, ex), device_id_type=MESH,
        )

    def m_copy(k):
        return pltpu.make_async_remote_copy(
            src_ref=norms2.at[0], dst_ref=norms2.at[k],
            send_sem=m_send.at[k], recv_sem=m_recv.at[k],
            device_id=(dp, (ex + k) % E), device_id_type=MESH,
        )

    for k in range(1, n):
        n_copy(k).start()
    for s in states:
        s.wait()
    total = norms[0]
    for k in range(1, n):
        n_copy(k).wait_recv()
        total = total + norms[k]
    norms2[0] = total
    for k in range(1, E):
        m_copy(k).start()
    for k in range(1, E):
        m_copy(k).wait_recv()
        total = total + norms2[k]
    clip_all = jnp.minimum(1.0, clip_limit / (jnp.sqrt(total) + norm_eps))
    clip_factor = jnp.max(clip_all)

    def g_copy(zz, c, way):
        where = lanes((zz * X + x) * share + c * chunk, chunk)
        if way < 2:
            target = at_dp(z + 1 if way == 0 else z - 1, x)
        else:
            target = at_dp(z, (x + way - 1) % X)
        return pltpu.make_async_remote_copy(
            src_ref=gathered.at[:, where], dst_ref=gathered.at[:, where],
            send_sem=g_send.at[way, zz, c], recv_sem=g_recv.at[zz * X + x, c],
            device_id=target, device_id_type=MESH,
        )

    def arrived(zz, xx, c):
        where = lanes((zz * X + xx) * share + c * chunk, chunk)
        pltpu.make_async_remote_copy(
            src_ref=gathered.at[:, where], dst_ref=gathered.at[:, where],
            send_sem=g_send.at[0, 0, c], recv_sem=g_recv.at[zz * X + xx, c],
            device_id=(dp, (ex + 1) % E), device_id_type=MESH,
        ).wait_recv()

    def put(zz, xx, c):
        where = lanes((zz * X + xx) * share + c * chunk, chunk)
        return pltpu.make_async_copy(
            gathered.at[:, where], params_out.at[:, where], p_sem.at[zz * X + xx, c]
        )

    outs = ((master, master_out), (first, first_out), (second, second_out))

    def out_copy(i, c):
        where = lanes(c * chunk, chunk)
        a, b = outs[i]
        return pltpu.make_async_copy(a.at[:, where], b.at[:, where], out_sem.at[i, c])

    def update(c, carry):
        def body(b, inner):
            where = lanes(c * chunk + b * BLOCK, BLOCK)
            m, f, s = adam_update(
                sbuf[z, :, where], master[:, where], first[:, where], second[:, where], clip_factor
            )
            master[:, where] = m
            first[:, where] = f
            second[:, where] = s
            gathered[:, lanes(dp * share + c * chunk + b * BLOCK, BLOCK)] = m.astype(jnp.bfloat16)
            return inner

        lax.fori_loop(0, chunk // BLOCK, body, 0)

        @pl.when(z < Z - 1)
        def _():
            g_copy(z, c, 0).start()

        @pl.when(z > 0)
        def _():
            g_copy(z, c, 1).start()

        for k in range(1, X):
            g_copy(z, c, k + 1).start()
        for i in range(3):
            out_copy(i, c).start()
        put(z, x, c).start()
        return carry

    lax.fori_loop(0, CHUNKS, update, 0)

    for s in range(1, Z):
        def relay(c, carry, s=s):
            @pl.when(z - s >= 0)
            def _():
                arrived(z - s, x, c)

                @pl.when(z < Z - 1)
                def _():
                    g_copy(z - s, c, 0).start()

                for k in range(1, X):
                    g_copy(z - s, c, k + 1).start()
                put(z - s, x, c).start()

            @pl.when(z + s < Z)
            def _():
                arrived(z + s, x, c)

                @pl.when(z > 0)
                def _():
                    g_copy(z + s, c, 1).start()

                for k in range(1, X):
                    g_copy(z + s, c, k + 1).start()
                put(z + s, x, c).start()

            return carry

        lax.fori_loop(0, CHUNKS, relay, 0)

    for s in range(Z):
        def collect(zz):
            def body(c, carry):
                for k in range(1, X):
                    arrived(zz, (x + k) % X, c)
                    put(zz, (x + k) % X, c).start()
                return carry

            lax.fori_loop(0, CHUNKS, body, 0)

        for_dest(s, collect)

    def drain(c, carry):
        for zz in range(Z):
            for k in range(1, X):
                x_copy(zz, k, c).wait_send()
                g_copy(zz, c, k + 1).wait_send()

            @pl.when(zz > z)
            def _():
                z_copy(zz, c, True).wait_send()

            @pl.when(zz < z)
            def _():
                z_copy(zz, c, False).wait_send()

            @pl.when(jnp.logical_and(zz <= z, z < Z - 1))
            def _():
                g_copy(zz, c, 0).wait_send()

            @pl.when(jnp.logical_and(zz >= z, z > 0))
            def _():
                g_copy(zz, c, 1).wait_send()

            for xx in range(X):
                put(zz, xx, c).wait()
        for i in range(3):
            out_copy(i, c).wait()
        return carry

    lax.fori_loop(0, CHUNKS, drain, 0)
    for k in range(1, n):
        n_copy(k).wait_send()
    for k in range(1, E):
        m_copy(k).wait_send()


def split(count):
    rows = 1
    while rows * rows < count:
        rows *= 2
    return rows, count // rows


def shards(Z, X, E, local_grads, master_weights, first_moment, second_moment):
    layers, flat = local_grads.shape[2:]
    n = Z * X
    share = flat // n
    whole = pl.BlockSpec(memory_space=pl.ANY)
    piece = jax.ShapeDtypeStruct((layers, share), F32)
    dma = pltpu.SemaphoreType.DMA
    state = pltpu.VMEM((layers, share), F32)
    results = pl.pallas_call(
        functools.partial(kernel, Z, X, E, share),
        out_shape=(jax.ShapeDtypeStruct((layers, flat), jnp.bfloat16), piece, piece, piece),
        in_specs=[whole] * 4,
        out_specs=(whole,) * 4,
        scratch_shapes=[
            pltpu.VMEM((Z, layers, share), jnp.bfloat16),
            pltpu.VMEM((Z, X - 1, layers, share), jnp.bfloat16),
            pltpu.VMEM((Z, layers, share), F32),
            pltpu.VMEM((Z, layers, share), F32),
            pltpu.VMEM((Z, layers, share), F32),
            state, state, state,
            pltpu.VMEM((layers, flat), jnp.bfloat16),
            pltpu.VMEM((n, 8, 128), F32),
            pltpu.VMEM((E, 8, 128), F32),
            dma((Z,)), dma((3,)), dma((3, CHUNKS)),
            dma((Z, X - 1, CHUNKS)), dma((Z, X - 1, CHUNKS)),
            dma((Z, CHUNKS)), dma((Z, CHUNKS)), dma((Z, CHUNKS)),
            dma((n,)), dma((n,)), dma((E,)), dma((E,)),
            dma((X + 1, Z, CHUNKS)), dma((n, CHUNKS)), dma((n, CHUNKS)),
        ],
        compiler_params=pltpu.CompilerParams(
            collective_id=0, has_side_effects=True, vmem_limit_bytes=60 * 1024 * 1024
        ),
    )(local_grads[0, 0], master_weights[0], first_moment[0], second_moment[0])
    return tuple(r[None] for r in results)


def solution(mesh):
    Z, X = split(mesh.shape["dp"])
    moments = P("expert", None, "dp")
    return jax.shard_map(
        functools.partial(shards, Z, X, mesh.shape["expert"]),
        mesh=mesh,
        in_specs=(P("dp", "expert", None, None), moments, moments, moments),
        out_specs=(P("expert", None, None), moments, moments, moments),
        check_vma=False,
    )
```

time: 240 us -> 145 us (0.60)
  blocking collectives: 139 us -> 0 us
  Pallas kernels: 0 us -> 136 us
  waiting for transfers between devices: 68.7 us -> 0 us
  between operations: 14.8 us -> 0.66 us
  other arithmetic: 11.2 us -> 0 us
  local copies, waits for them, and re-layouts: 5.29 us -> 8.35 us
    pallas_call x0 -> x1, Pallas kernels: none -> 136 us  [shards(): pl.pallas_call(functools.partial(kernel, Z, X, E, share), out_shape=(jax....]
    all_to_all x1 -> x0, blocking collectives: 100 us -> none  [shards(): lax.all_to_all(pieces_all, 'dp', split_axis=1, concat_axis=1, tiled=True)]
    all_gather x1 -> x0, waiting for transfers between devices: 68.7 us -> none  [shards(): gathered = lax.all_gather(rounded, 'dp', axis=1, tiled=True)]
    psum x1 -> x0, blocking collectives: 38.9 us -> none  [shards(): total_squares = lax.psum(squares, ('dp', 'expert'))]
    sub x1 -> x0, other arithmetic: 4.45 us -> none  [adam_update(): new_master = master - learn_rate * (decay_rate * master + direction)]
    convert_element_type x1 -> x0, other arithmetic: 3.72 us -> none  [shards(): rounded = new_master.astype(jnp.bfloat16)]
    unnamed x5 -> x10, local copies, waits for them, and re-layouts: 5.29 us -> 8.35 us
    reduce_sum x2 -> x0, other arithmetic: 3 us -> none  [the longest x1 1.86 us: shards(): reduced = jnp.sum(arrived.astype(jnp.float32), axis=1)]
  transfers between devices with their start and end apart: 1 -> 0, of which waited for: 1 -> 0; matrix products, arithmetic and copies ran while one was open for 2% -> 0% of each run, Pallas kernels for 0% -> 0%
where the time goes in v1:
time: 145 us
  Pallas kernels  136 us (94%)
  local copies, waits for them, and re-layouts  8.35 us (6%)
    pallas_call x1, Pallas kernels, shards(): pl.pallas_call(functools.partial(kernel, Z, X, E, share), out_shape=(jax....  136 us
    unnamed x10, local copies, waits for them, and re-layouts  8.35 us

profile of v1, /device:TPU:0, one launch (start us, length us, event | category | flops | bytes accessed | tf_op | source)
XLA Modules:
  0.0 144.6 jit_solution(10718948850621083425)
XLA Ops:
  0.6 135.6 %shard_map.75 = (bf16[4,524288]{1,0:T(4,128)(2,1)}, f32[4,65536]{1,0:T(4,128)}, f32[4,65536]{1,0:T(4,128)}, f32[4,65536]{1,0:T(4,128)}) custom-call(bf16[4,524288]{1,0:T(4,128)(2,1)} %bitcast.8, f32[4,65536]{1,0:T(4,128)} %bitcast.10, f32[4,65536]{1,0:T(4,128)} %bitcast.11, f32[4,65536]{1,0:T(4,128)} %bitcast.12), custom_call_target="tpu_custom_call" | custom-call | tf_op jit(solution)/shard_map/pallas_call | solution.py:396
  136.3 0.0 copy-start.2
  136.3 0.0 copy-start.1
  136.3 5.4 %copy.12 = bf16[1,4,524288]{2,1,0:T(4,128)(2,1)} copy(bf16[1,4,524288]{2,1,0:T(4,128)(2,1)} %bitcast.9) | data formatting | bytes 8388608
  141.7 0.0 copy-done.2
  141.7 0.0 copy-start
  141.7 1.0 copy.13
  142.7 0.0 copy-done.1
  142.7 1.0 copy.14
  143.7 0.0 copy-done
  143.7 1.0 copy.15
Async XLA Ops:
  136.3 5.5 %copy-start.2 = (f32[4,65536]{1,0:T(4,128)S(1)}, f32[4,65536]{1,0:T(4,128)}, u32[]{:S(2)}) copy-start(f32[4,65536]{1,0:T(4,128)} %get-tuple-element.9) | copy-start | bytes 3145732
  136.3 6.4 %copy-start.1 = (f32[4,65536]{1,0:T(4,128)S(1)}, f32[4,65536]{1,0:T(4,128)}, u32[]{:S(2)}) copy-start(f32[4,65536]{1,0:T(4,128)} %get-tuple-element.10) | copy-start | bytes 3145732
  141.7 1.9 %copy-start = (f32[4,65536]{1,0:T(4,128)S(1)}, f32[4,65536]{1,0:T(4,128)}, u32[]{:S(2)}) copy-start(f32[4,65536]{1,0:T(4,128)} %get-tuple-element.11) | copy-start | bytes 3145732

commit v2 on v1

--- a/solution.py
+++ b/solution.py
@@ -19,7 +19,10 @@
 
 MESH = pl.DeviceIdType.MESH
 F32 = jnp.float32
-CHUNKS = 4
+CHUNKS = 8
+HALF = CHUNKS // 2
+PIECES = 8
+SPARE_BYTES = 4 * 1024 * 1024
 BLOCK = 2048
 
 
@@ -35,10 +38,10 @@
 def kernel(
     Z, X, E, share,
     grads, master_in, first_in, second_in,
-    params_out, master_out, first_out, second_out,
-    own, xr, low, high, sbuf, master, first, second, gathered, norms, norms2,
-    own_sem, state_sem, out_sem, x_send, x_recv, z_send, low_recv, high_recv,
-    n_send, n_recv, m_send, m_recv, g_send, g_recv, p_sem,
+    gathered, master, first, second,
+    xr, low, high, sbuf, norms, norms2,
+    x_send, x_recv, z_send, low_recv, high_recv,
+    n_send, n_recv, m_send, m_recv, g_send, g_recv, h_send,
 ):
     n = Z * X
     dp = lax.axis_index("dp")
@@ -59,11 +62,6 @@
         pl.semaphore_signal(barrier, inc=1, device_id=(dp, (ex + k) % E), device_id_type=MESH)
     pl.semaphore_wait(barrier, n - 1 + E - 1)
 
-    def own_copy(zz):
-        return pltpu.make_async_copy(
-            grads.at[:, lanes((zz * X + x) * share, share)], own.at[zz], own_sem.at[zz]
-        )
-
     def x_copy(zz, k, c):
         to = (x + k) % X
         return pltpu.make_async_remote_copy(
@@ -86,8 +84,6 @@
                 act(z - k)
 
     def start_first(zz):
-        own_copy(zz).start()
-
         def body(c, carry):
             for k in range(1, X):
                 x_copy(zz, k, c).start()
@@ -97,13 +93,6 @@
 
     for k in range(Z - 1, -1, -1):
         for_dest(k, start_first)
-    states = [
-        pltpu.make_async_copy(a, b, state_sem.at[i])
-        for i, (a, b) in enumerate(((master_in, master), (first_in, first), (second_in, second)))
-    ]
-    for s in states:
-        s.start()
-
     def z_copy(zz, c, up):
         where = lanes(c * chunk, chunk)
         return pltpu.make_async_remote_copy(
@@ -115,8 +104,9 @@
             device_id_type=MESH,
         )
 
-    def sum_block(zz, where, extras):
-        total = own[zz, :, where].astype(F32)
+    def sum_block(zz, at, extras):
+        where = lanes(at, BLOCK)
+        total = grads[:, lanes((zz * X + x) * share + at, BLOCK)].astype(F32)
         for k in range(1, X):
             total = total + xr[zz, k - 1, :, where].astype(F32)
         for r in extras:
@@ -125,8 +115,8 @@
 
     def add_chunk(zz, c, extras):
         def body(b, carry):
-            where = lanes(c * chunk + b * BLOCK, BLOCK)
-            sbuf[zz, :, where] = sum_block(zz, where, extras)
+            at = c * chunk + b * BLOCK
+            sbuf[zz, :, lanes(at, BLOCK)] = sum_block(zz, at, extras)
             return carry
 
         lax.fori_loop(0, chunk // BLOCK, body, 0)
@@ -148,8 +138,6 @@
         z_copy(zz, c, up).start()
 
     for k in range(Z - 1, 0, -1):
-        for_dest(k, lambda zz: own_copy(zz).wait())
-
         def body(c, carry, k=k):
             @pl.when(z + k < Z)
             def _():
@@ -163,17 +151,16 @@
 
         lax.fori_loop(0, CHUNKS, body, 0)
 
-    own_copy(z).wait()
     norms2[0] = jnp.zeros((8, 128), F32)
 
     def finish_chunk(c, extras):
         def body(b, carry):
-            where = lanes(c * chunk + b * BLOCK, BLOCK)
-            mean = sum_block(z, where, extras) / n
-            sbuf[z, :, where] = mean
+            at = c * chunk + b * BLOCK
+            mean = sum_block(z, at, extras) / n
+            sbuf[z, :, lanes(at, BLOCK)] = mean
             return carry + mean * mean
 
-        squares = lax.fori_loop(0, chunk // BLOCK, body, jnp.zeros((own.shape[1], BLOCK), F32))
+        squares = lax.fori_loop(0, chunk // BLOCK, body, jnp.zeros((grads.shape[0], BLOCK), F32))
         norms2[0] = norms2[0] + jnp.full((8, 128), jnp.sum(squares), F32)
 
     def finish(c, carry):
@@ -222,8 +209,6 @@
 
     for k in range(1, n):
         n_copy(k).start()
-    for s in states:
-        s.wait()
     total = norms[0]
     for k in range(1, n):
         n_copy(k).wait_recv()
@@ -257,24 +242,27 @@
             device_id=(dp, (ex + 1) % E), device_id_type=MESH,
         ).wait_recv()
 
-    def put(zz, xx, c):
-        where = lanes((zz * X + xx) * share + c * chunk, chunk)
-        return pltpu.make_async_copy(
-            gathered.at[:, where], params_out.at[:, where], p_sem.at[zz * X + xx, c]
-        )
-
-    outs = ((master, master_out), (first, first_out), (second, second_out))
-
-    def out_copy(i, c):
-        where = lanes(c * chunk, chunk)
-        a, b = outs[i]
-        return pltpu.make_async_copy(a.at[:, where], b.at[:, where], out_sem.at[i, c])
+    pair = z + 1 - 2 * (z % 2)
+
+    def h_copy(k, c):
+        where = lanes((z * X + (x + k) % X) * share + c * chunk, chunk)
+        return pltpu.make_async_remote_copy(
+            src_ref=gathered.at[:, where], dst_ref=gathered.at[:, where],
+            send_sem=h_send.at[k - 1, c], recv_sem=g_recv.at[z * X + (x + k) % X, c],
+            device_id=at_dp(pair, x), device_id_type=MESH,
+        )
+
+    def along_x(zz, c, act):
+        @pl.when(jnp.logical_or(zz != pair, c < HALF))
+        def _():
+            for k in range(1, X):
+                act(g_copy(zz, c, k + 1))
 
     def update(c, carry):
         def body(b, inner):
             where = lanes(c * chunk + b * BLOCK, BLOCK)
             m, f, s = adam_update(
-                sbuf[z, :, where], master[:, where], first[:, where], second[:, where], clip_factor
+                sbuf[z, :, where], master_in[:, where], first_in[:, where], second_in[:, where], clip_factor
             )
             master[:, where] = m
             first[:, where] = f
@@ -294,9 +282,6 @@
 
         for k in range(1, X):
             g_copy(z, c, k + 1).start()
-        for i in range(3):
-            out_copy(i, c).start()
-        put(z, x, c).start()
         return carry
 
     lax.fori_loop(0, CHUNKS, update, 0)
@@ -311,9 +296,7 @@
                 def _():
                     g_copy(z - s, c, 0).start()
 
-                for k in range(1, X):
-                    g_copy(z - s, c, k + 1).start()
-                put(z - s, x, c).start()
+                along_x(z - s, c, lambda copy: copy.start())
 
             @pl.when(z + s < Z)
             def _():
@@ -323,23 +306,29 @@
                 def _():
                     g_copy(z + s, c, 1).start()
 
+                along_x(z + s, c, lambda copy: copy.start())
+
+            return carry
+
+        lax.fori_loop(0, CHUNKS, relay, 0)
+
+        if s == 1:
+            def across(c, carry):
                 for k in range(1, X):
-                    g_copy(z + s, c, k + 1).start()
-                put(z + s, x, c).start()
-
-            return carry
-
-        lax.fori_loop(0, CHUNKS, relay, 0)
+                    arrived(z, (x + k) % X, c)
+                    h_copy(k, c).start()
+                return carry
+
+            lax.fori_loop(HALF, CHUNKS, across, 0)
 
     for s in range(Z):
-        def collect(zz):
+        def collect(zz, s=s):
             def body(c, carry):
                 for k in range(1, X):
                     arrived(zz, (x + k) % X, c)
-                    put(zz, (x + k) % X, c).start()
                 return carry
 
-            lax.fori_loop(0, CHUNKS, body, 0)
+            lax.fori_loop(0, HALF if s == 0 else CHUNKS, body, 0)
 
         for_dest(s, collect)
 
@@ -347,7 +336,7 @@
         for zz in range(Z):
             for k in range(1, X):
                 x_copy(zz, k, c).wait_send()
-                g_copy(zz, c, k + 1).wait_send()
+            along_x(zz, c, lambda copy: copy.wait_send())
 
             @pl.when(zz > z)
             def _():
@@ -365,10 +354,11 @@
             def _():
                 g_copy(zz, c, 1).wait_send()
 
-            for xx in range(X):
-                put(zz, xx, c).wait()
-        for i in range(3):
-            out_copy(i, c).wait()
+        @pl.when(c >= HALF)
+        def _():
+            for k in range(1, X):
+                h_copy(k, c).wait_send()
+
         return carry
 
     lax.fori_loop(0, CHUNKS, drain, 0)
@@ -378,6 +368,23 @@
         m_copy(k).wait_send()
 
 
+def write_out(count, *refs):
+    sources, targets, sem = refs[:count], refs[count : 2 * count], refs[2 * count]
+
+    def copies(i):
+        size = sources[i].shape[1] // PIECES
+        for p in range(PIECES):
+            where = pl.ds(p * size, size)
+            yield pltpu.make_async_copy(sources[i].at[:, where], targets[i].at[:, where], sem.at[i, p])
+
+    for i in range(count):
+        for copy in copies(i):
+            copy.start()
+    for i in range(count):
+        for copy in copies(i):
+            copy.wait()
+
+
 def split(count):
     rows = 1
     while rows * rows < count:
@@ -389,35 +396,42 @@
     layers, flat = local_grads.shape[2:]
     n = Z * X
     share = flat // n
-    whole = pl.BlockSpec(memory_space=pl.ANY)
+    whole = pl.BlockSpec(memory_space=pltpu.HBM)
     piece = jax.ShapeDtypeStruct((layers, share), F32)
     dma = pltpu.SemaphoreType.DMA
-    state = pltpu.VMEM((layers, share), F32)
+    local = pl.BlockSpec(memory_space=pltpu.VMEM)
+    shapes = (jax.ShapeDtypeStruct((layers, flat), jnp.bfloat16), piece, piece, piece)
+    out_bytes = layers * (2 * flat + 3 * 4 * share)
+    used_bytes = layers * Z * share * (2 * X + 3 * 4) + 2 * out_bytes
     results = pl.pallas_call(
         functools.partial(kernel, Z, X, E, share),
-        out_shape=(jax.ShapeDtypeStruct((layers, flat), jnp.bfloat16), piece, piece, piece),
-        in_specs=[whole] * 4,
-        out_specs=(whole,) * 4,
+        out_shape=shapes,
+        in_specs=[local] * 4,
+        out_specs=(local,) * 4,
         scratch_shapes=[
-            pltpu.VMEM((Z, layers, share), jnp.bfloat16),
             pltpu.VMEM((Z, X - 1, layers, share), jnp.bfloat16),
             pltpu.VMEM((Z, layers, share), F32),
             pltpu.VMEM((Z, layers, share), F32),
             pltpu.VMEM((Z, layers, share), F32),
-            state, state, state,
-            pltpu.VMEM((layers, flat), jnp.bfloat16),
             pltpu.VMEM((n, 8, 128), F32),
             pltpu.VMEM((E, 8, 128), F32),
-            dma((Z,)), dma((3,)), dma((3, CHUNKS)),
             dma((Z, X - 1, CHUNKS)), dma((Z, X - 1, CHUNKS)),
             dma((Z, CHUNKS)), dma((Z, CHUNKS)), dma((Z, CHUNKS)),
             dma((n,)), dma((n,)), dma((E,)), dma((E,)),
-            dma((X + 1, Z, CHUNKS)), dma((n, CHUNKS)), dma((n, CHUNKS)),
+            dma((X + 1, Z, CHUNKS)), dma((n, CHUNKS)), dma((X - 1, CHUNKS)),
         ],
         compiler_params=pltpu.CompilerParams(
-            collective_id=0, has_side_effects=True, vmem_limit_bytes=60 * 1024 * 1024
+            collective_id=0, has_side_effects=True, vmem_limit_bytes=used_bytes + SPARE_BYTES
         ),
     )(local_grads[0, 0], master_weights[0], first_moment[0], second_moment[0])
+    results = pl.pallas_call(
+        functools.partial(write_out, len(shapes)),
+        out_shape=shapes,
+        in_specs=[local] * 4,
+        out_specs=(whole,) * 4,
+        scratch_shapes=[dma((len(shapes), PIECES))],
+        compiler_params=pltpu.CompilerParams(vmem_limit_bytes=out_bytes + SPARE_BYTES),
+    )(*results)
     return tuple(r[None] for r in results)
 
 

time: 145 us -> 142 us (0.979)
  local copies, waits for them, and re-layouts: 8.35 us -> 5.85 us
    unnamed x10 -> x8, local copies, waits for them, and re-layouts: 8.35 us -> 5.85 us
    pallas_call x1 -> x2, Pallas kernels: 136 us -> 135 us  [the longest x1 132 us: shards(): pl.pallas_call(functools.partial(kernel, Z, X, E, share), out_shape=shape...]
where the time goes in v2:
time: 142 us; the launch traced here: 141 us
  Pallas kernels  135 us (95%)
  local copies, waits for them, and re-layouts  5.85 us (4%)
    pallas_call x1, Pallas kernels, shards(): pl.pallas_call(functools.partial(kernel, Z, X, E, share), out_shape=shape...  132 us
    unnamed x8, local copies, waits for them, and re-layouts  5.85 us
    pallas_call x1, Pallas kernels, shards(): pl.pallas_call(functools.partial(write_out, len(shapes)), out_shape=shape...  3.22 us

profile of v2, /device:TPU:0, one launch (start us, length us, event | category | flops | bytes accessed | tf_op | source)
XLA Modules:
  0.0 141.4 jit_solution(4452716436338151983)
XLA Ops:
  0.6 0.0 copy-start
  0.6 2.2 %copy-done = bf16[1,1,4,524288]{3,2,1,0:T(4,128)(2,1)S(1)} copy-done((bf16[1,1,4,524288]{3,2,1,0:T(4,128)(2,1)S(1)}, bf16[1,1,4,524288]{3,2,1,0:T(4,128)(2,1)}, u32[]{:S(2)}) %copy-start) | copy-done | bytes 4194328
  2.8 0.0 copy-start.1
  2.8 1.2 copy-done.1
  4.0 0.0 copy-start.2
  4.0 1.2 copy-done.2
  5.3 0.0 copy-start.3
  5.3 1.2 copy-done.3
  6.5 131.7 %shard_map.75 = (bf16[4,524288]{1,0:T(4,128)(2,1)S(1)}, f32[4,65536]{1,0:T(4,128)S(1)}, f32[4,65536]{1,0:T(4,128)S(1)}, f32[4,65536]{1,0:T(4,128)S(1)}) custom-call(bf16[4,524288]{1,0:T(4,128)(2,1)S(1)} %bitcast.8, f32[4,65536]{1,0:T(4,128)S(1)} %bitcast.9, f32[4,65536]{1,0:T(4,128)S(1)} %bitcast.10, f32[4,65536]{1,0:T(4,128)S(1)} %bitcast.11), custom_call_target="tpu_custom_call" | custom-call | tf_op jit(solution)/shard_map/pallas_call | solution.py:406
  138.2 3.2 %shard_map.76 = (bf16[4,524288]{1,0:T(4,128)(2,1)}, f32[4,65536]{1,0:T(4,128)}, f32[4,65536]{1,0:T(4,128)}, f32[4,65536]{1,0:T(4,128)}) custom-call(bf16[4,524288]{1,0:T(4,128)(2,1)S(1)} %get-tuple-element.12.refs_0_, f32[4,65536]{1,0:T(4,128)S(1)} %get-tuple-element.13.refs_1_, f32[4,65536]{1,0:T(4,128)S(1)} %get-tuple-element.14.refs_2_, ...), custom_call_target="tpu_custom_call" | custom-call | tf_op jit(solution)/shard_map/pallas_call | solution.py:427
Async XLA Ops:
  0.6 2.2 %copy-start = (bf16[1,1,4,524288]{3,2,1,0:T(4,128)(2,1)S(1)}, bf16[1,1,4,524288]{3,2,1,0:T(4,128)(2,1)}, u32[]{:S(2)}) copy-start(bf16[1,1,4,524288]{3,2,1,0:T(4,128)(2,1)} %param.4) | copy-start | bytes 12582916
  2.8 1.2 copy-start.1
  4.0 1.2 copy-start.2
  5.3 1.2 copy-start.3

commit v3 on v2

--- a/solution.py
+++ b/solution.py
@@ -39,8 +39,8 @@
     Z, X, E, share,
     grads, master_in, first_in, second_in,
     gathered, master, first, second,
-    xr, low, high, sbuf, norms, norms2,
-    x_send, x_recv, z_send, low_recv, high_recv,
+    own, xr, low, high, sbuf, norms, norms2,
+    own_sem, state_sem, x_send, x_recv, z_send, low_recv, high_recv,
     n_send, n_recv, m_send, m_recv, g_send, g_recv, h_send,
 ):
     n = Z * X
@@ -62,6 +62,11 @@
         pl.semaphore_signal(barrier, inc=1, device_id=(dp, (ex + k) % E), device_id_type=MESH)
     pl.semaphore_wait(barrier, n - 1 + E - 1)
 
+    def own_copy(zz):
+        return pltpu.make_async_copy(
+            grads.at[:, lanes((zz * X + x) * share, share)], own.at[zz], own_sem.at[zz]
+        )
+
     def x_copy(zz, k, c):
         to = (x + k) % X
         return pltpu.make_async_remote_copy(
@@ -84,6 +89,8 @@
                 act(z - k)
 
     def start_first(zz):
+        own_copy(zz).start()
+
         def body(c, carry):
             for k in range(1, X):
                 x_copy(zz, k, c).start()
@@ -93,6 +100,13 @@
 
     for k in range(Z - 1, -1, -1):
         for_dest(k, start_first)
+    states = [
+        pltpu.make_async_copy(a, b, state_sem.at[i])
+        for i, (a, b) in enumerate(((master_in, master), (first_in, first), (second_in, second)))
+    ]
+    for s in states:
+        s.start()
+
     def z_copy(zz, c, up):
         where = lanes(c * chunk, chunk)
         return pltpu.make_async_remote_copy(
@@ -104,9 +118,8 @@
             device_id_type=MESH,
         )
 
-    def sum_block(zz, at, extras):
-        where = lanes(at, BLOCK)
-        total = grads[:, lanes((zz * X + x) * share + at, BLOCK)].astype(F32)
+    def sum_block(zz, where, extras):
+        total = own[zz, :, where].astype(F32)
         for k in range(1, X):
             total = total + xr[zz, k - 1, :, where].astype(F32)
         for r in extras:
@@ -115,8 +128,8 @@
 
     def add_chunk(zz, c, extras):
         def body(b, carry):
-            at = c * chunk + b * BLOCK
-            sbuf[zz, :, lanes(at, BLOCK)] = sum_block(zz, at, extras)
+            where = lanes(c * chunk + b * BLOCK, BLOCK)
+            sbuf[zz, :, where] = sum_block(zz, where, extras)
             return carry
 
         lax.fori_loop(0, chunk // BLOCK, body, 0)
@@ -138,6 +151,8 @@
         z_copy(zz, c, up).start()
 
     for k in range(Z - 1, 0, -1):
+        for_dest(k, lambda zz: own_copy(zz).wait())
+
         def body(c, carry, k=k):
             @pl.when(z + k < Z)
             def _():
@@ -151,16 +166,17 @@
 
         lax.fori_loop(0, CHUNKS, body, 0)
 
+    own_copy(z).wait()
     norms2[0] = jnp.zeros((8, 128), F32)
 
     def finish_chunk(c, extras):
         def body(b, carry):
-            at = c * chunk + b * BLOCK
-            mean = sum_block(z, at, extras) / n
-            sbuf[z, :, lanes(at, BLOCK)] = mean
+            where = lanes(c * chunk + b * BLOCK, BLOCK)
+            mean = sum_block(z, where, extras) / n
+            sbuf[z, :, where] = mean
             return carry + mean * mean
 
-        squares = lax.fori_loop(0, chunk // BLOCK, body, jnp.zeros((grads.shape[0], BLOCK), F32))
+        squares = lax.fori_loop(0, chunk // BLOCK, body, jnp.zeros((own.shape[1], BLOCK), F32))
         norms2[0] = norms2[0] + jnp.full((8, 128), jnp.sum(squares), F32)
 
     def finish(c, carry):
@@ -209,6 +225,8 @@
 
     for k in range(1, n):
         n_copy(k).start()
+    for s in states:
+        s.wait()
     total = norms[0]
     for k in range(1, n):
         n_copy(k).wait_recv()
@@ -262,7 +280,7 @@
         def body(b, inner):
             where = lanes(c * chunk + b * BLOCK, BLOCK)
             m, f, s = adam_update(
-                sbuf[z, :, where], master_in[:, where], first_in[:, where], second_in[:, where], clip_factor
+                sbuf[z, :, where], master[:, where], first[:, where], second[:, where], clip_factor
             )
             master[:, where] = m
             first[:, where] = f
@@ -401,20 +419,23 @@
     dma = pltpu.SemaphoreType.DMA
     local = pl.BlockSpec(memory_space=pltpu.VMEM)
     shapes = (jax.ShapeDtypeStruct((layers, flat), jnp.bfloat16), piece, piece, piece)
+    arrays = (local_grads[0, 0], master_weights[0], first_moment[0], second_moment[0])
     out_bytes = layers * (2 * flat + 3 * 4 * share)
-    used_bytes = layers * Z * share * (2 * X + 3 * 4) + 2 * out_bytes
+    used_bytes = layers * Z * share * (2 * X + 3 * 4) + out_bytes
     results = pl.pallas_call(
         functools.partial(kernel, Z, X, E, share),
         out_shape=shapes,
-        in_specs=[local] * 4,
+        in_specs=[whole] * 4,
         out_specs=(local,) * 4,
         scratch_shapes=[
+            pltpu.VMEM((Z, layers, share), jnp.bfloat16),
             pltpu.VMEM((Z, X - 1, layers, share), jnp.bfloat16),
             pltpu.VMEM((Z, layers, share), F32),
             pltpu.VMEM((Z, layers, share), F32),
             pltpu.VMEM((Z, layers, share), F32),
             pltpu.VMEM((n, 8, 128), F32),
             pltpu.VMEM((E, 8, 128), F32),
+            dma((Z,)), dma((3,)),
             dma((Z, X - 1, CHUNKS)), dma((Z, X - 1, CHUNKS)),
             dma((Z, CHUNKS)), dma((Z, CHUNKS)), dma((Z, CHUNKS)),
             dma((n,)), dma((n,)), dma((E,)), dma((E,)),
@@ -423,7 +444,7 @@
         compiler_params=pltpu.CompilerParams(
             collective_id=0, has_side_effects=True, vmem_limit_bytes=used_bytes + SPARE_BYTES
         ),
-    )(local_grads[0, 0], master_weights[0], first_moment[0], second_moment[0])
+    )(*(pltpu.with_memory_space_constraint(a, pltpu.HBM) for a in arrays))
     results = pl.pallas_call(
         functools.partial(write_out, len(shapes)),
         out_shape=shapes,

time: 142 us -> 136 us (0.958)
  local copies, waits for them, and re-layouts: 5.85 us -> 0 us
    unnamed x8 -> x0, local copies, waits for them, and re-layouts: 5.85 us -> none
where the time goes in v3:
time: 136 us
  Pallas kernels  135 us (99%)
    pallas_call x1, Pallas kernels, shards(): pl.pallas_call(functools.partial(kernel, Z, X, E, share), out_shape=shape...  132 us
    pallas_call x1, Pallas kernels, shards(): pl.pallas_call(functools.partial(write_out, len(shapes)), out_shape=shape...  3.22 us

profile of v3, /device:TPU:0, one launch (start us, length us, event | category | flops | bytes accessed | tf_op | source)
XLA Modules:
  0.0 136.0 jit_solution(15331523162908453137)
XLA Ops:
  0.6 132.2 %shard_map.75 = (bf16[4,524288]{1,0:T(4,128)(2,1)S(1)}, f32[4,65536]{1,0:T(4,128)S(1)}, f32[4,65536]{1,0:T(4,128)S(1)}, f32[4,65536]{1,0:T(4,128)S(1)}) custom-call(bf16[4,524288]{1,0:T(4,128)(2,1)} %bitcast.8, f32[4,65536]{1,0:T(4,128)} %bitcast.9, f32[4,65536]{1,0:T(4,128)} %bitcast.10, f32[4,65536]{1,0:T(4,128)} %bitcast.11), custom_call_target="tpu_custom_call" | custom-call | tf_op jit(solution)/shard_map/pallas_call | solution.py:425
  132.8 3.2 %shard_map.76 = (bf16[4,524288]{1,0:T(4,128)(2,1)}, f32[4,65536]{1,0:T(4,128)}, f32[4,65536]{1,0:T(4,128)}, f32[4,65536]{1,0:T(4,128)}) custom-call(bf16[4,524288]{1,0:T(4,128)(2,1)S(1)} %get-tuple-element.12.refs_0_, f32[4,65536]{1,0:T(4,128)S(1)} %get-tuple-element.13.refs_1_, f32[4,65536]{1,0:T(4,128)S(1)} %get-tuple-element.14.refs_2_, ...), custom_call_target="tpu_custom_call" | custom-call | tf_op jit(solution)/shard_map/pallas_call | solution.py:448

commit v4 on v3

--- a/solution.py
+++ b/solution.py
@@ -19,7 +19,7 @@
 
 MESH = pl.DeviceIdType.MESH
 F32 = jnp.float32
-CHUNKS = 8
+CHUNKS = 16
 HALF = CHUNKS // 2
 PIECES = 8
 SPARE_BYTES = 4 * 1024 * 1024

time: 136 us -> 138 us (1.015)
  Pallas kernels: 135 us -> 137 us
    pallas_call x1, Pallas kernels: 132 us -> 134 us  [shards(): pl.pallas_call(functools.partial(kernel, Z, X, E, share), out_shape=shape...]
where the time goes in v4:
time: 138 us
  Pallas kernels  137 us (99%)
    pallas_call x1, Pallas kernels, shards(): pl.pallas_call(functools.partial(kernel, Z, X, E, share), out_shape=shape...  134 us
    pallas_call x1, Pallas kernels, shards(): pl.pallas_call(functools.partial(write_out, len(shapes)), out_shape=shape...  3.22 us

profile of v4, /device:TPU:0, one launch (start us, length us, event | category | flops | bytes accessed | tf_op | source)
XLA Modules:
  0.0 137.9 jit_solution(5537495162651580143)
XLA Ops:
  0.6 134.0 %shard_map.75 = (bf16[4,524288]{1,0:T(4,128)(2,1)S(1)}, f32[4,65536]{1,0:T(4,128)S(1)}, f32[4,65536]{1,0:T(4,128)S(1)}, f32[4,65536]{1,0:T(4,128)S(1)}) custom-call(bf16[4,524288]{1,0:T(4,128)(2,1)} %bitcast.8, f32[4,65536]{1,0:T(4,128)} %bitcast.9, f32[4,65536]{1,0:T(4,128)} %bitcast.10, f32[4,65536]{1,0:T(4,128)} %bitcast.11), custom_call_target="tpu_custom_call" | custom-call | tf_op jit(solution)/shard_map/pallas_call | solution.py:425
  134.7 3.2 %shard_map.76 = (bf16[4,524288]{1,0:T(4,128)(2,1)}, f32[4,65536]{1,0:T(4,128)}, f32[4,65536]{1,0:T(4,128)}, f32[4,65536]{1,0:T(4,128)}) custom-call(bf16[4,524288]{1,0:T(4,128)(2,1)S(1)} %get-tuple-element.12.refs_0_, f32[4,65536]{1,0:T(4,128)S(1)} %get-tuple-element.13.refs_1_, f32[4,65536]{1,0:T(4,128)S(1)} %get-tuple-element.14.refs_2_, ...), custom_call_target="tpu_custom_call" | custom-call | tf_op jit(solution)/shard_map/pallas_call | solution.py:448
